TPU v7x, 32 devices: a whole 2x2x4 slice. The times are simulated.
32 devices in a mesh: sx: 4 (over y, x), sy: 8 (over z, core).
Axes of the slice: x: 2, y: 2, z: 4, core: 2. Of those that a mesh axis runs over, the one named last changes fastest.
Arguments:
- collocation: float32 [2, 4, 2048], P(None, 'sx', 'sy'), may hold values from -1 to 1
- source: float32 [4, 2048], P('sx', 'sy'), may hold values from -31.5 to 40.5
- wall_index: int32 [4, 4, 512], P(None, 'sx', 'sy'), may hold values from 0 to 1023, as said below
- bc_type: int32 [2, 8], P(None, 'sy'), may hold values from 0 to 1
- bc_value: float32 [2, 512], P(None, 'sy'), may hold values from -4 to 4
- in_weight: float32 [4, 3, 4096], P('sx', None, 'sy'), may hold values from -4 to 4
- local_weight: bfloat16 [4, 512, 4096], P('sx', None, 'sy'), may hold values from -0.25 to 0.25
- local_bias: float32 [4, 4096], P('sx', 'sy'), may hold values from -3 to 3
- trunk_weight: bfloat16 [1, 512, 512], replicated, may hold values from -0.25 to 0.25
- trunk_bias: float32 [1, 512], replicated, may hold values from -3 to 3
- head_weight: float32 [4, 4096], P('sx', 'sy'), may hold values from -0.25 to 0.25
Outputs:
- trunk_grad: float32 [1, 512, 512], replicated
- trunk_bias_grad: float32 [1, 512], replicated
- in_grad: float32 [4, 3, 4096], P('sx', None, 'sy')
- local_grad: float32 [4, 512, 4096], P('sx', None, 'sy')
- local_bias_grad: float32 [4, 4096], P('sx', 'sy')
- head_grad: float32 [4, 4096], P('sx', 'sy')
- loss_value: float32 [], replicated
Inputs may be any that keep to these rules, and one draw needn't show every extreme that they name: `wall_index`: within a wall the positions are distinct. A shared wall has the same positions on both sides: wall 0 of (i, j) equals wall 1 of (i - 1, j), and wall 2 of (i, j) equals wall 3 of (i, (j - 1) mod 8).
All inputs are finite; a program needn't handle non-finite values.
Results may differ from a plain program's by a relative error of at most 0.0016.
Values sent between devices are 32-bit elements; how exact they have to be, the bound alone decides.
No kernel may reach another device: no remote copies, remote signals or barrier semaphores. Data moves between devices by JAX's collectives and lax.ppermute only.
A program may use at most 64 MiB of HBM per device.

v0:
```python
import jax
import jax.numpy as jnp
from jax import lax
from jax.sharding import PartitionSpec as P

SLOTS = 1024
HIGH = lax.Precision.HIGHEST
EPS = 1e-06


def extended(x, sides, width, wrap):
    for axis, dim in sides:
        size, length = (lax.axis_size(axis), x.shape[dim])
        up = [(i, (i + 1) % size) for i in range(size if wrap else size - 1)]
        down = [(j, i) for i, j in up]
        last = lax.slice_in_dim(x, length - width, length, axis=dim)
        initial = lax.slice_in_dim(x, 0, width, axis=dim)
        before = lax.ppermute(last, axis, up)
        after = lax.ppermute(initial, axis, down)
        x = jnp.concatenate([before, x, after], axis=dim)
    return x


def activate(preact):
    values = jnp.tanh(preact[0])
    slopes = 1.0 - values * values
    result = [values, slopes * preact[1]]
    if preact.shape[0] == 5:
        curvature = -2.0 * values * slopes
        result.append(slopes * preact[2])
        result.append(slopes * preact[3] + curvature * preact[1] * preact[1])
        result.append(slopes * preact[4] + curvature * preact[2] * preact[2])
    return jnp.stack(result)


def entry_streams(coords, in_weight, directions):
    preact = coords[0][:, None] * in_weight[0] + coords[1][:, None] * in_weight[1] + in_weight[2]
    streams = [preact] + [
        jnp.broadcast_to(2.0 * in_weight[direction], preact.shape) for direction in directions
    ]
    if len(directions) == 2:
        streams = streams + [jnp.zeros_like(preact), jnp.zeros_like(preact)]
    return jnp.stack(streams)


def layer_list(params):
    layers = [(params[1], params[2])]
    layers.append((params[3][0], params[4][0]))
    return layers


def run_forward(coords, directions, params):
    preact = entry_streams(coords, params[0], directions)
    activity, pullback = jax.vjp(activate, preact)
    pullbacks = [pullback]
    lowered = []
    for weight, layer_bias in layer_list(params):
        lowered_in = activity.astype(jnp.bfloat16)
        lowered.append(lowered_in)
        stream_count, row_count, breadth = lowered_in.shape
        product = jnp.dot(
            lowered_in.reshape(stream_count * row_count, breadth),
            weight,
            preferred_element_type=jnp.float32,
        )
        preact = product.reshape(stream_count, row_count, -1)
        preact = preact.at[0].add(layer_bias)
        activity, pullback = jax.vjp(activate, preact)
        pullbacks.append(pullback)
    outputs = jnp.dot(activity, params[5], precision=HIGH)
    return (outputs, (activity, lowered, pullbacks))


def run_backward(coords, directions, params, tape, cotangent):
    activity, lowered, pullbacks = tape
    layers = layer_list(params)
    head_grad = jnp.einsum("kr,krw->w", cotangent, activity, precision=HIGH)
    upstream = cotangent[:, :, None] * params[5]
    weight_grads = []
    bias_grads = []
    for layer_index in reversed(range(len(layers))):
        (preact_grad,) = pullbacks[layer_index + 1](upstream)
        lowered_grad = preact_grad.astype(jnp.bfloat16)
        stream_count, row_count, breadth = lowered_grad.shape
        flat_grad = lowered_grad.reshape(stream_count * row_count, breadth)
        flat_input = lowered[layer_index].reshape(stream_count * row_count, -1)
        weight_grads.insert(
            0,
            lax.dot_general(
                flat_input, flat_grad, (((0,), (0,)), ((), ())), preferred_element_type=jnp.float32
            ),
        )
        bias_grads.insert(0, jnp.sum(preact_grad[0], axis=0))
        upstream = lax.dot_general(
            flat_grad,
            layers[layer_index][0],
            (((1,), (1,)), ((), ())),
            preferred_element_type=jnp.float32,
        ).reshape(stream_count, row_count, -1)
    (entry_grad,) = pullbacks[0](upstream)
    in_grad = jnp.concatenate(
        [jnp.dot(coords, entry_grad[0], precision=HIGH), jnp.sum(entry_grad[0], axis=0)[None]],
        axis=0,
    )
    for stream, direction in enumerate(directions):
        in_grad = in_grad.at[direction].add(2.0 * jnp.sum(entry_grad[1 + stream], axis=0))
    return (
        in_grad,
        weight_grads[0],
        bias_grads[0],
        jnp.stack(weight_grads[1:]),
        jnp.stack(bias_grads[1:]),
        head_grad,
    )


def wall_coords(wall_slots, slot_total):
    spots = (2.0 * wall_slots.astype(jnp.float32) + 1.0) / slot_total - 1.0
    unit_row = jnp.ones_like(spots[0])
    x_coords = jnp.stack(
        [jnp.concatenate([-unit_row, unit_row]), jnp.concatenate([spots[0], spots[1]])]
    )
    y_coords = jnp.stack(
        [jnp.concatenate([spots[2], spots[3]]), jnp.concatenate([-unit_row, unit_row])]
    )
    return (x_coords, y_coords)


def to_rims(outputs):
    half_size = outputs.shape[1] // 2
    return outputs.reshape(2, 2, half_size).transpose(1, 0, 2).reshape(2, 2 * half_size)


def residual_sum(outputs, forcing):
    residual = outputs[3] + outputs[4] + forcing
    return jnp.sum(residual * residual)


def wall_misfit(own_data, neighbour, target, bc_flag, is_outer, normal):
    half_size = own_data.shape[0] // 2
    interface = jnp.sum((own_data - neighbour) ** 2)
    dirichlet = jnp.sum((own_data[:half_size] - target) ** 2)
    neumann = jnp.sum((normal * own_data[half_size:] - target) ** 2)
    boundary = jnp.where(bc_flag == 0, dirichlet, neumann)
    return jnp.where(is_outer, boundary, interface)


def x_misfit(x_rims, neighbours, targets, bc_flags, at_start, at_end):
    return wall_misfit(
        x_rims[0], neighbours[0], targets[0], bc_flags[0], at_start, -1.0
    ) + wall_misfit(x_rims[1], neighbours[1], targets[1], bc_flags[1], at_end, 1.0)


def y_misfit(y_rims, neighbours):
    return jnp.sum((y_rims - neighbours) ** 2)


def blend(inner_grads, wall_grads, inner_factor, wall_factor):
    return tuple(
        (
            inner_factor * inner_part + wall_factor * wall_part
            for inner_part, wall_part in zip(inner_grads, wall_grads)
        )
    )


def per_device(
    collocation,
    source,
    wall_index,
    bc_type,
    bc_value,
    in_weight,
    local_weight,
    local_bias,
    trunk_weight,
    trunk_bias,
    head_weight,
):
    params = (
        in_weight[0],
        local_weight[0],
        local_bias[0],
        trunk_weight,
        trunk_bias,
        head_weight[0],
    )
    points = collocation[:, 0, :]
    forcing = source[0]
    x_coords, y_coords = wall_coords(wall_index[:, 0, :], SLOTS)
    x_out, x_tape = run_forward(x_coords, (0,), params)
    y_out, y_tape = run_forward(y_coords, (1,), params)
    x_rims = to_rims(x_out)
    y_rims = to_rims(y_out)
    x_padded = extended(x_rims, (("sx", 0),), 1, False)
    y_padded = extended(y_rims, (("sy", 0),), 1, True)
    inner_out, inner_tape = run_forward(points, (0, 1), params)
    residual_total, inner_cotangent = jax.value_and_grad(residual_sum)(inner_out, forcing)
    row_place = lax.axis_index("sx")
    at_start = row_place == 0
    at_end = row_place == lax.axis_size("sx") - 1
    x_total, x_rim_grad = jax.value_and_grad(x_misfit)(
        x_rims, jnp.stack([x_padded[0], x_padded[3]]), bc_value, bc_type[:, 0], at_start, at_end
    )
    y_total, y_rim_grad = jax.value_and_grad(y_misfit)(
        y_rims, jnp.stack([y_padded[0], y_padded[3]])
    )
    wall_total = x_total + y_total
    inner_grads = run_backward(points, (0, 1), params, inner_tape, inner_cotangent)
    x_grads = run_backward(x_coords, (0,), params, x_tape, to_rims(x_rim_grad))
    y_grads = run_backward(y_coords, (1,), params, y_tape, to_rims(y_rim_grad))
    wall_grads = tuple(
        (first_part + second_part for first_part, second_part in zip(x_grads, y_grads))
    )
    devices_all = lax.axis_size("sx") * lax.axis_size("sy")
    inner_count = points.shape[1] * devices_all
    wall_count = 4 * wall_index.shape[2] * devices_all
    gathered = lax.psum(
        (residual_total, wall_total, inner_grads[3], inner_grads[4], wall_grads[3], wall_grads[4]),
        ("sx", "sy"),
    )
    inner_mean = gathered[0] / inner_count
    wall_mean = gathered[1] / wall_count
    balance_weight = jnp.sqrt((wall_mean + EPS) / (inner_mean + EPS))
    combined = blend(inner_grads, wall_grads, balance_weight / inner_count, 1.0 / wall_count)
    trunk_grad, trunk_bias_grad = blend(
        (gathered[2], gathered[3]),
        (gathered[4], gathered[5]),
        balance_weight / inner_count,
        1.0 / wall_count,
    )
    loss_value = balance_weight * inner_mean + wall_mean
    return (
        trunk_grad,
        trunk_bias_grad,
        combined[0][None],
        combined[1][None],
        combined[2][None],
        combined[5][None],
        loss_value,
    )


def solution(mesh):
    return jax.shard_map(
        per_device,
        mesh=mesh,
        in_specs=(
            P(None, "sx", "sy"),
            P("sx", "sy"),
            P(None, "sx", "sy"),
            P(None, "sy"),
            P(None, "sy"),
            P("sx", None, "sy"),
            P("sx", None, "sy"),
            P("sx", "sy"),
            P(),
            P(),
            P("sx", "sy"),
        ),
        out_specs=(
            P(),
            P(),
            P("sx", None, "sy"),
            P("sx", None, "sy"),
            P("sx", "sy"),
            P("sx", "sy"),
            P(),
        ),
        check_vma=False,
    )
```

profile of v0, /device:TPU:0, one launch (start us, length us, event | category | flops | bytes accessed | tf_op | source)
XLA Modules:
  0.0 322.9 jit_solution(16296578300917998260)
XLA Ops:
  9.7 1.5 fusion.68
  11.2 1.3 fusion.66
  19.8 1.3 slice.443
  21.2 6.0 %collective-permute-start = (f32[1,128]{1,0:T(1,128)}, f32[1,128]{1,0:T(1,128)}, u32[]{:S(2)}, u32[]{:S(2)}) collective-permute-start(f32[1,128]{1,0:T(1,128)} %slice.443), channel_id=1, source_target_pairs={{0,8},{8,16},{16,24},{1,9},{9,17},{17,25},{2,10},{10,18},{18,26},{... | collective-permute-start | bytes 1544 | tf_op jit(solution)/shard_map/ppermute | solution.py:18
  27.2 1.4 fusion.26
  31.0 3.0 collective-permute-start.3
  34.0 1.3 slice.458
  48.5 2.3 fusion.150
  53.8 2.0 fusion.190
  55.8 1.9 convolution_bitcast_fusion.5
  60.0 1.9 fusion.188
  66.2 3.7 %fusion.145 = f32[1,512,1]{1,0,2:T(1,128)} fusion(f32[5,256,512]{2,1,0:T(8,128)} %copy-done.2, f32[5,256,1]{1,0,2:T(8,128)} %get-tuple-element.247), kind=kOutput, calls=%fused_computation.294 | convolution fusion | flops 7864320 | bytes 2628608 | tf_op jit(solution)/shard_map/kr,krw->w/dot_general | solution.py:77
  69.9 1.7 slice_reduce_fusion.3
  71.6 1.6 slice_reduce_fusion
  77.6 2.0 multiply_reduce_fusion.4
  82.3 1.3 scatter-add.15
  85.7 1.3 reshape.1820
  89.6 1.3 mul.1249
  91.4 1.7 reduce.49
  94.5 1.8 reduce.50
  99.4 1.3 reshape.1855
  100.7 1.3 mul.1260
  110.3 1.8 reduce.52
  113.4 1.8 reduce.51
  120.3 39.4 %all-reduce.47 = (f32[]{:T(128)}, f32[]{:T(128)}, f32[1,512]{1,0:T(1,128)}, f32[1,512]{1,0:T(1,128)}) all-reduce(f32[]{:T(128)S(6)} %add.491, f32[]{:T(128)} %get-tuple-element.162, f32[1,512]{1,0:T(1,128)S(1)} %bitcast.531, f32[1,512]{1,0:T(1,128)} %bitcast.529), channel_id=1, replica_groups=mesh['sx'=4,'sy'=8] {'sx','sy'}, use_global_device_ids=true, to_apply=%region_7.0 | all-reduce | flops 1026 | bytes 8208 | tf_op jit(solution)/shard_map/psum | solution.py:218
  161.2 2.0 fusion.30
  163.2 1.9 fusion.34
  166.4 2.4 convolution_bitcast_fusion
  180.6 1.6 fusion.6
  182.2 1.8 fusion.2
  184.0 128.1 %all-reduce.51.cloned.1.call-done = (f32[1,512,512]{2,1,0:T(8,128)}, f32[1,512,512]{2,1,0:T(8,128)}) async-done(((f32[1,512,512]{2,1,0:T(8,128)}, f32[1,512,512]{2,1,0:T(8,128)}), (f32[1,512,512]{2,1,0:T(8,128)}, f32[1,512,512]{2,1,0:T(8,128)})) %all-reduce.51.cloned.1.call-update) | async-done | bytes 2097168 | tf_op jit(solution)/shard_map/psum | solution.py:218
  312.2 2.7 multiply_add_fusion
  (229 shorter events, 72.8 us)
Async XLA Ops:
  7.2 5.6 %copy-start = (bf16[1,512,512]{2,1,0:T(8,128)(2,1)S(1)}, bf16[1,512,512]{2,1,0:T(8,128)(2,1)}, u32[]{:S(2)}) copy-start(bf16[1,512,512]{2,1,0:T(8,128)(2,1)} %param.39) | copy-start | bytes 1572868
  7.2 5.4 %copy-start.28 = (f32[1,512]{1,0:T(1,128)S(1)}, f32[1,512]{1,0:T(1,128)}, u32[]{:S(2)}) copy-start(f32[1,512]{1,0:T(1,128)} %param.38) | copy-start | bytes 6148
  7.2 305.0 %all-reduce.51.cloned.1.call-start = ((), (), s32[]{:S(2)}) async-start(), calls=%async_computation | async-start | bytes 4194304 | tf_op jit(solution)/shard_map/psum | solution.py:218
  8.7 3.8 %copy-start.31 = (f32[512]{0:T(512)}, f32[512]{0:T(512)S(1)}, u32[]{:S(2)}) copy-start(f32[512]{0:T(512)S(1)} %get-tuple-element.253) | copy-start | bytes 6148
  8.7 3.8 %copy-start.34 = (f32[512]{0:T(512)}, f32[512]{0:T(512)S(1)}, u32[]{:S(2)}) copy-start(f32[512]{0:T(512)S(1)} %get-tuple-element.254) | copy-start | bytes 6148
  8.8 3.8 %copy-start.48 = (f32[128]{0:T(128)}, f32[128]{0:T(128)S(1)}, u32[]{:S(2)}) copy-start(f32[128]{0:T(128)S(1)} %get-tuple-element.251) | copy-start | bytes 1540
  8.8 3.8 %copy-start.50 = (f32[128]{0:T(128)}, f32[128]{0:T(128)S(1)}, u32[]{:S(2)}) copy-start(f32[128]{0:T(128)S(1)} %get-tuple-element.252) | copy-start | bytes 1540
  9.7 3.4 %copy-start.17 = (bf16[1,128,512]{2,1,0:T(8,128)(2,1)}, bf16[1,128,512]{2,1,0:T(8,128)(2,1)S(1)}, u32[]{:S(2)}) copy-start(bf16[1,128,512]{2,1,0:T(8,128)(2,1)S(1)} %get-tuple-element.215) | copy-start | bytes 393220
  13.1 30.0 %copy-start.6 = (f32[2,128,512]{2,1,0:T(8,128)}, f32[2,128,512]{2,1,0:T(8,128)S(1)}, u32[]{:S(2)}) copy-start(f32[2,128,512]{2,1,0:T(8,128)S(1)} %fusion.56) | copy-start | bytes 1572868
  13.7 31.3 %copy-start.1 = (bf16[1,512,512]{2,1,0:T(8,128)(2,1)S(1)}, bf16[1,512,512]{2,1,0:T(8,128)(2,1)}, u32[]{:S(2)}) copy-start(bf16[1,512,512]{2,1,0:T(8,128)(2,1)} %param.37) | copy-start | bytes 1572868
  14.7 31.2 %copy-start.3 = (f32[1,128,512]{2,1,0:T(8,128)}, f32[1,128,512]{2,1,0:T(8,128)S(1)}, u32[]{:S(2)}) copy-start(f32[1,128,512]{2,1,0:T(8,128)S(1)} %get-tuple-element.238) | copy-start | bytes 786436
  14.7 31.2 %copy-start.4 = (f32[1,128,512]{2,1,0:T(8,128)}, f32[1,128,512]{2,1,0:T(8,128)S(1)}, u32[]{:S(2)}) copy-start(f32[1,128,512]{2,1,0:T(8,128)S(1)} %get-tuple-element.169) | copy-start | bytes 786436
  14.7 31.2 %copy-start.12 = (f32[1,128,512]{2,1,0:T(8,128)}, f32[1,128,512]{2,1,0:T(8,128)S(1)}, u32[]{:S(2)}) copy-start(f32[1,128,512]{2,1,0:T(8,128)S(1)} %get-tuple-element.237) | copy-start | bytes 786436
  18.6 65.0 %collective-permute-start.1 = (f32[1,128]{1,0:T(1,128)}, f32[1,128]{1,0:T(1,128)}, u32[]{:S(2)}, u32[]{:S(2)}) collective-permute-start(f32[1,128]{1,0:T(1,128)} %slice.450), channel_id=1, source_target_pairs={{8,0},{16,8},{24,16},{9,1},{17,9},{25,17},{10,2},{18,10},{26,18},{... | collective-permute-start | bytes 1544 | tf_op jit(solution)/shard_map/ppermute | solution.py:19
  21.2 63.2 %collective-permute-start = (f32[1,128]{1,0:T(1,128)}, f32[1,128]{1,0:T(1,128)}, u32[]{:S(2)}, u32[]{:S(2)}) collective-permute-start(f32[1,128]{1,0:T(1,128)} %slice.443), channel_id=1, source_target_pairs={{0,8},{8,16},{16,24},{1,9},{9,17},{17,25},{2,10},{10,18},{18,26},{... | collective-permute-start | bytes 1544 | tf_op jit(solution)/shard_map/ppermute | solution.py:18
  31.0 59.9 %collective-permute-start.3 = (f32[1,128]{1,0:T(1,128)}, f32[1,128]{1,0:T(1,128)}, u32[]{:S(2)}, u32[]{:S(2)}) collective-permute-start(f32[1,128]{1,0:T(1,128)} %slice.460), channel_id=1, source_target_pairs={{1,0},{2,1},{3,2},{4,3},{5,4},{6,5},{7,6},{0,7},{9,8},{10,9},{11,1... | collective-permute-start | bytes 1544 | tf_op jit(solution)/shard_map/ppermute | solution.py:19
  35.3 59.2 %collective-permute-start.2 = (f32[1,128]{1,0:T(1,128)}, f32[1,128]{1,0:T(1,128)}, u32[]{:S(2)}, u32[]{:S(2)}) collective-permute-start(f32[1,128]{1,0:T(1,128)} %slice.458), channel_id=1, source_target_pairs={{0,1},{1,2},{2,3},{3,4},{4,5},{5,6},{6,7},{7,0},{8,9},{9,10},{10,1... | collective-permute-start | bytes 1544 | tf_op jit(solution)/shard_map/ppermute | solution.py:18
  48.5 3.6 %copy-start.2 = (f32[5,256,512]{2,1,0:T(8,128)}, f32[5,256,512]{2,1,0:T(8,128)S(1)}, u32[]{:S(2)}) copy-start(f32[5,256,512]{2,1,0:T(8,128)S(1)} %add_dynamic-update-slice_fusion) | copy-start | bytes 7864324
  66.2 7.0 %copy-start.47 = (f32[512]{0:T(512)S(1)}, f32[512]{0:T(512)}, u32[]{:S(2)}) copy-start(f32[512]{0:T(512)} %get-tuple-element.141) | copy-start | bytes 6148
  66.2 7.6 %copy-start.46 = (f32[512]{0:T(512)S(1)}, f32[512]{0:T(512)}, u32[]{:S(2)}) copy-start(f32[512]{0:T(512)} %get-tuple-element.143) | copy-start | bytes 6148
  66.2 7.6 %copy-start.42 = (f32[2,512]{1,0:T(2,128)S(1)}, f32[2,512]{1,0:T(2,128)}, u32[]{:S(2)}) copy-start(f32[2,512]{1,0:T(2,128)} %convolution_bitcast_fusion.6) | copy-start | bytes 12292
  66.2 8.2 %copy-start.44 = (f32[512]{0:T(512)S(1)}, f32[512]{0:T(512)}, u32[]{:S(2)}) copy-start(f32[512]{0:T(512)} %get-tuple-element.142) | copy-start | bytes 6148
  107.3 9.2 %copy-start.41 = (f32[1,2,2,64]{3,1,2,0:T(2,128)S(1)}, f32[1,2,2,64]{3,1,2,0:T(2,128)}, u32[]{:S(2)}) copy-start(f32[1,2,2,64]{3,1,2,0:T(2,128)} %copy-done.40) | copy-start | bytes 3076
  161.1 7.7 %copy-start.14 = (bf16[2,128,512]{2,1,0:T(8,128)(2,1)S(1)}, bf16[2,128,512]{2,1,0:T(8,128)(2,1)}, u32[]{:S(2)}) copy-start(bf16[2,128,512]{2,1,0:T(8,128)(2,1)} %fusion.10) | copy-start | bytes 786436
  161.1 8.0 %copy-start.33 = (f32[512]{0:T(512)S(1)}, f32[512]{0:T(512)}, u32[]{:S(2)}) copy-start(f32[512]{0:T(512)} %copy-done.31) | copy-start | bytes 6148
  161.1 8.0 %copy-start.36 = (f32[512]{0:T(512)S(1)}, f32[512]{0:T(512)}, u32[]{:S(2)}) copy-start(f32[512]{0:T(512)} %copy-done.34) | copy-start | bytes 6148
  161.1 8.0 %copy-start.49 = (f32[128]{0:T(128)S(1)}, f32[128]{0:T(128)}, u32[]{:S(2)}) copy-start(f32[128]{0:T(128)} %copy-done.48) | copy-start | bytes 1540
  161.1 8.0 %copy-start.51 = (f32[128]{0:T(128)S(1)}, f32[128]{0:T(128)}, u32[]{:S(2)}) copy-start(f32[128]{0:T(128)} %copy-done.50) | copy-start | bytes 1540
  161.2 8.0 %copy-start.52 = (f32[128]{0:T(128)S(1)}, f32[128]{0:T(128)}, u32[]{:S(2)}) copy-start(f32[128]{0:T(128)} %constant.271.clone.1) | copy-start | bytes 1540
  169.6 5.8 %copy-start.39 = (f32[3,512]{1,0:T(4,128)S(1)}, f32[3,512]{1,0:T(4,128)}, u32[]{:S(2)}) copy-start(f32[3,512]{1,0:T(4,128)} %scatter-add.15) | copy-start | bytes 18436
  170.5 10.0 %copy-start.9 = (bf16[2,128,512]{2,1,0:T(8,128)(2,1)S(1)}, bf16[2,128,512]{2,1,0:T(8,128)(2,1)}, u32[]{:S(2)}) copy-start(bf16[2,128,512]{2,1,0:T(8,128)(2,1)} %fusion.9) | copy-start | bytes 786436
  173.3 8.9 %copy-start.16 = (bf16[5,256,512]{2,1,0:T(8,128)(2,1)S(1)}, bf16[5,256,512]{2,1,0:T(8,128)(2,1)}, u32[]{:S(2)}) copy-start(bf16[5,256,512]{2,1,0:T(8,128)(2,1)} %copy-done.15) | copy-start | bytes 3932164
  (28 other events, 52.1 us)
Sparse Core Ops, SparseCore 0:
  176.9 135.2 all-reduce.50
where the time goes:
time: 325 us; the launch traced here: 323 us
  waiting for transfers between devices  128 us (39%)
  other arithmetic  54.6 us (17%)
  blocking collectives  39.4 us (12%)
  local copies, waits for them, and re-layouts  35.2 us (11%)
  matrix products  31.9 us (10%)
  between operations  23.3 us (7%)
  starting transfers between devices  10.3 us (3%)
    psum x1, waiting for transfers between devices, per_device(): lax.psum((residual_total, wall_total, inner_grads[3], inner_grads[4], wal...  128 us
    psum x1, blocking collectives, per_device(): lax.psum((residual_total, wall_total, inner_grads[3], inner_grads[4], wal...  39.4 us
    dot_general x6, matrix products, run_backward(): lax.dot_general(flat_input, flat_grad, (((0,), (0,)), ((), ())), preferre...  9.33 us
    dot_general x3, matrix products, run_backward(): head_grad = jnp.einsum('kr,krw->w', cotangent, activity, precision=HIGH)  7.62 us
    add x4, other arithmetic, blend(): inner_factor * inner_part + wall_factor * wall_part  6.55 us
  transfers between devices with their start and end apart: 5, of which 1 were waited for; matrix products, arithmetic and copies ran while one was open for 21% of the time, Pallas kernels for 0%

commit v1 on v0

--- a/solution.py
+++ b/solution.py
@@ -216,8 +216,18 @@
     inner_count = points.shape[1] * devices_all
     wall_count = 4 * wall_index.shape[2] * devices_all
     gathered = lax.psum(
-        (residual_total, wall_total, inner_grads[3], inner_grads[4], wall_grads[3], wall_grads[4]),
-        ("sx", "sy"),
+        lax.psum(
+            (
+                residual_total,
+                wall_total,
+                inner_grads[3],
+                inner_grads[4],
+                wall_grads[3],
+                wall_grads[4],
+            ),
+            "sy",
+        ),
+        "sx",
     )
     inner_mean = gathered[0] / inner_count
     wall_mean = gathered[1] / wall_count

time: 325 us -> 254 us (0.78)
  waiting for transfers between devices: 128 us -> 88.5 us
  blocking collectives: 39.4 us -> 28.6 us
  local copies, waits for them, and re-layouts: 35.2 us -> 25.7 us
  other arithmetic: 54.6 us -> 49 us
  matrix products: 31.9 us -> 26.8 us
    psum x1, waiting for transfers between devices: 128 us -> 26.4 us  [per_device(): lax.psum((residual_total, wall_total, inner_grads[3], inner_grads[4], wal...]
    psum x0 -> x1, waiting for transfers between devices: none -> 62 us  [per_device(): lax.psum(lax.psum((residual_total, wall_total, inner_grads[3], inner_grad...]
    psum x1, blocking collectives: 39.4 us -> 18.6 us  [per_device(): lax.psum((residual_total, wall_total, inner_grads[3], inner_grads[4], wal...]
    psum x0 -> x1, blocking collectives: none -> 10 us  [per_device(): lax.psum(lax.psum((residual_total, wall_total, inner_grads[3], inner_grad...]
  transfers between devices with their start and end apart: 5 -> 6, of which waited for: 1 -> 2; matrix products, arithmetic and copies ran while one was open for 21% -> 29% of each run, Pallas kernels for 0% -> 0%
where the time goes in v1:
time: 254 us; the launch traced here: 252 us
  waiting for transfers between devices  88.5 us (35%)
  other arithmetic  49 us (19%)
  blocking collectives  28.6 us (11%)
  matrix products  26.8 us (11%)
  local copies, waits for them, and re-layouts  25.7 us (10%)
  between operations  23.5 us (9%)
  starting transfers between devices  10.4 us (4%)
    psum x1, waiting for transfers between devices, per_device(): lax.psum(lax.psum((residual_total, wall_total, inner_grads[3], inner_grad...  62 us
    psum x1, waiting for transfers between devices, per_device(): lax.psum((residual_total, wall_total, inner_grads[3], inner_grads[4], wal...  26.4 us
    psum x1, blocking collectives, per_device(): lax.psum((residual_total, wall_total, inner_grads[3], inner_grads[4], wal...  18.6 us
    psum x1, blocking collectives, per_device(): lax.psum(lax.psum((residual_total, wall_total, inner_grads[3], inner_grad...  10 us
    reduce_sum x6, other arithmetic, run_backward(): bias_grads.insert(0, jnp.sum(preact_grad[0], axis=0))  7.3 us
    dot_general x6, matrix products, run_backward(): lax.dot_general(flat_input, flat_grad, (((0,), (0,)), ((), ())), preferre...  7 us
    ppermute x2, starting transfers between devices, extended(): before = lax.ppermute(last, axis, up)  6.01 us
    mul x4, local copies, waits for them, and re-layouts, run_backward(): upstream = cotangent[:, :, None] * params[5]  5.33 us
  transfers between devices with their start and end apart: 6, of which 2 were waited for; matrix products, arithmetic and copies ran while one was open for 29% of the time, Pallas kernels for 0%

profile of v1, /device:TPU:0, one launch (start us, length us, event | category | flops | bytes accessed | tf_op | source)
XLA Modules:
  0.0 252.3 jit_solution(4866765783376346382)
XLA Ops:
  9.7 1.5 fusion.68
  11.2 1.3 fusion.66
  18.3 6.0 %collective-permute-start = (f32[1,128]{1,0:T(1,128)}, f32[1,128]{1,0:T(1,128)}, u32[]{:S(2)}, u32[]{:S(2)}) collective-permute-start(f32[1,128]{1,0:T(1,128)} %slice.443), channel_id=1, source_target_pairs={{0,8},{8,16},{16,24},{1,9},{9,17},{17,25},{2,10},{10,18},{18,26},{... | collective-permute-start | bytes 1544 | tf_op jit(solution)/shard_map/ppermute | solution.py:18
  25.7 3.0 %collective-permute-start.3 = (f32[1,128]{1,0:T(1,128)}, f32[1,128]{1,0:T(1,128)}, u32[]{:S(2)}, u32[]{:S(2)}) collective-permute-start(f32[1,128]{1,0:T(1,128)} %slice.460), channel_id=1, source_target_pairs={{1,0},{2,1},{3,2},{4,3},{5,4},{6,5},{7,6},{0,7},{9,8},{10,9},{11,1... | collective-permute-start | bytes 1544 | tf_op jit(solution)/shard_map/ppermute | solution.py:19
  37.0 2.3 fusion.150
  42.3 2.1 fusion.190
  44.3 1.8 convolution_bitcast_fusion.5
  48.4 1.8 fusion.188
  54.7 3.7 %fusion.145 = f32[1,512,1]{1,0,2:T(1,128)} fusion(f32[5,256,512]{2,1,0:T(8,128)} %copy-done.2, f32[5,256,1]{1,0,2:T(8,128)} %get-tuple-element.253), kind=kOutput, calls=%fused_computation.294 | convolution fusion | flops 7864320 | bytes 2628608 | tf_op jit(solution)/shard_map/kr,krw->w/dot_general | solution.py:77
  58.4 1.7 slice_reduce_fusion.3
  60.1 1.7 slice_reduce_fusion
  63.5 1.3 scatter-add.14
  66.1 2.0 multiply_reduce_fusion.4
  70.7 1.3 scatter-add.15
  74.7 1.7 reduce.52
  77.7 1.8 reduce.51
  80.8 1.3 reshape.1820
  83.4 1.3 mul.1249
  84.7 1.8 reduce.49
  87.8 1.8 reduce.50
  89.7 1.3 stack.111
  91.0 1.3 multiply_reduce_fusion
  92.9 1.3 mul.1260
  108.0 18.6 %all-reduce.47 = (f32[]{:T(128)}, f32[]{:T(128)}, f32[1,512]{1,0:T(1,128)S(1)}, f32[1,512]{1,0:T(1,128)S(1)}) all-reduce(f32[]{:T(128)S(6)} %add.503, f32[]{:T(128)} %get-tuple-element.168, f32[1,512]{1,0:T(1,128)S(1)} %bitcast.532, f32[1,512]{1,0:T(1,128)} %bitcast.529), channel_id=1, replica_groups=mesh['sx'=4,'sy'=8] {'sy'}, use_global_device_ids=true, to_apply=%region_7.0 | all-reduce | flops 1026 | bytes 8208 | tf_op jit(solution)/shard_map/psum | solution.py:219
  126.6 10.0 %all-reduce.49 = (f32[]{:T(128)}, f32[]{:T(128)}, f32[1,512]{1,0:T(1,128)}, f32[1,512]{1,0:T(1,128)}) all-reduce(f32[]{:T(128)} %get-tuple-element.154, f32[]{:T(128)} %get-tuple-element.155, f32[1,512]{1,0:T(1,128)S(1)} %get-tuple-element.156, f32[1,512]{1,0:T(1,128)S(1)} %get-tuple-element.157), channel_id=1, replica_groups=mesh['sx'=4,'sy'=8] {'sx'}, use_global_device_ids=true, to_apply=%region_8.0 | all-reduce | flops 1026 | bytes 8208 | tf_op jit(solution)/shard_map/psum | solution.py:218
  136.6 1.3 reshape.1853
  137.9 1.3 reshape.1855
  142.9 26.4 %all-reduce.54.cloned.1.call-done = (f32[1,512,512]{2,1,0:T(8,128)}, f32[1,512,512]{2,1,0:T(8,128)}) async-done(((f32[1,512,512]{2,1,0:T(8,128)}, f32[1,512,512]{2,1,0:T(8,128)}), (f32[1,512,512]{2,1,0:T(8,128)}, f32[1,512,512]{2,1,0:T(8,128)})) %all-reduce.54.cloned.1.call-update) | async-done | bytes 2097168 | tf_op jit(solution)/shard_map/psum | solution.py:219
  172.9 1.4 convolution_bitcast_fusion
  177.8 1.8 fusion.2
  179.7 62.0 %all-reduce.56.cloned.1.call-done = (f32[1,512,512]{2,1,0:T(8,128)}, f32[1,512,512]{2,1,0:T(8,128)}) async-done(((f32[1,512,512]{2,1,0:T(8,128)}, f32[1,512,512]{2,1,0:T(8,128)}), (f32[1,512,512]{2,1,0:T(8,128)}, f32[1,512,512]{2,1,0:T(8,128)})) %all-reduce.56.cloned.1.call-update) | async-done | bytes 2097168 | tf_op jit(solution)/shard_map/psum | solution.py:218
  241.6 2.7 %multiply_add_fusion = f32[1,512,512]{2,1,0:T(8,128)} fusion(f32[1,512,512]{2,1,0:T(8,128)} %get-tuple-element.164, f32[1,512,512]{2,1,0:T(8,128)} %get-tuple-element.165, f32[]{:T(128)S(6)} %div.27), kind=kLoop, calls=%fused_computation.18 | loop fusion | flops 786432 | bytes 3145732 | tf_op jit(solution)/shard_map/add | solution.py:161
  (273 shorter events, 57.9 us)
Async XLA Ops:
  7.2 5.6 %copy-start = (bf16[1,512,512]{2,1,0:T(8,128)(2,1)S(1)}, bf16[1,512,512]{2,1,0:T(8,128)(2,1)}, u32[]{:S(2)}) copy-start(bf16[1,512,512]{2,1,0:T(8,128)(2,1)} %param.39) | copy-start | bytes 1572868
  7.2 162.2 %all-reduce.54.cloned.1.call-start = ((), (), s32[]{:S(2)}) async-start(), calls=%async_computation | async-start | bytes 4194304 | tf_op jit(solution)/shard_map/psum | solution.py:219
  8.7 24.3 %copy-start.45 = (f32[512]{0:T(512)}, f32[512]{0:T(512)S(1)}, u32[]{:S(2)}) copy-start(f32[512]{0:T(512)S(1)} %get-tuple-element.260) | copy-start | bytes 6148
  8.7 24.6 %copy-start.42 = (f32[512]{0:T(512)}, f32[512]{0:T(512)S(1)}, u32[]{:S(2)}) copy-start(f32[512]{0:T(512)S(1)} %get-tuple-element.259) | copy-start | bytes 6148
  12.8 16.6 %copy-start.71 = (s32[2,1]{0,1:T(1,128)S(1)}, s32[2,1]{0,1:T(1,128)}, u32[]{:S(2)}) copy-start(s32[2,1]{0,1:T(1,128)} %param.34) | copy-start | bytes 28
  12.8 19.6 %copy-start.57 = (f32[2,1,256]{2,1,0:T(1,128)S(1)}, f32[2,1,256]{2,1,0:T(1,128)}, u32[]{:S(2)}) copy-start(f32[2,1,256]{2,1,0:T(1,128)} %param.31) | copy-start | bytes 6148
  13.7 20.0 %copy-start.1 = (bf16[1,512,512]{2,1,0:T(8,128)(2,1)S(1)}, bf16[1,512,512]{2,1,0:T(8,128)(2,1)}, u32[]{:S(2)}) copy-start(bf16[1,512,512]{2,1,0:T(8,128)(2,1)} %param.37) | copy-start | bytes 1572868
  13.9 20.6 %copy-start.3 = (f32[1,128,512]{2,1,0:T(8,128)}, f32[1,128,512]{2,1,0:T(8,128)S(1)}, u32[]{:S(2)}) copy-start(f32[1,128,512]{2,1,0:T(8,128)S(1)} %get-tuple-element.244) | copy-start | bytes 786436
  13.9 20.6 %copy-start.13 = (f32[1,128,512]{2,1,0:T(8,128)}, f32[1,128,512]{2,1,0:T(8,128)S(1)}, u32[]{:S(2)}) copy-start(f32[1,128,512]{2,1,0:T(8,128)S(1)} %get-tuple-element.243) | copy-start | bytes 786436
  16.5 55.6 %collective-permute-start.1 = (f32[1,128]{1,0:T(1,128)}, f32[1,128]{1,0:T(1,128)}, u32[]{:S(2)}, u32[]{:S(2)}) collective-permute-start(f32[1,128]{1,0:T(1,128)} %slice.450), channel_id=1, source_target_pairs={{8,0},{16,8},{24,16},{9,1},{17,9},{25,17},{10,2},{18,10},{26,18},{... | collective-permute-start | bytes 1544 | tf_op jit(solution)/shard_map/ppermute | solution.py:19
  18.3 54.5 %collective-permute-start = (f32[1,128]{1,0:T(1,128)}, f32[1,128]{1,0:T(1,128)}, u32[]{:S(2)}, u32[]{:S(2)}) collective-permute-start(f32[1,128]{1,0:T(1,128)} %slice.443), channel_id=1, source_target_pairs={{0,8},{8,16},{16,24},{1,9},{9,17},{17,25},{2,10},{10,18},{18,26},{... | collective-permute-start | bytes 1544 | tf_op jit(solution)/shard_map/ppermute | solution.py:18
  25.1 9.5 %copy-start.54 = (f32[1,2,2,64]{3,0,2,1:T(1,128)}, f32[1,2,2,64]{3,0,2,1:T(1,128)S(1)}, u32[]{:S(2)}) copy-start(f32[1,2,2,64]{3,0,2,1:T(1,128)S(1)} %fusion.26) | copy-start | bytes 3076
  25.7 59.0 %collective-permute-start.3 = (f32[1,128]{1,0:T(1,128)}, f32[1,128]{1,0:T(1,128)}, u32[]{:S(2)}, u32[]{:S(2)}) collective-permute-start(f32[1,128]{1,0:T(1,128)} %slice.460), channel_id=1, source_target_pairs={{1,0},{2,1},{3,2},{4,3},{5,4},{6,5},{7,6},{0,7},{9,8},{10,9},{11,1... | collective-permute-start | bytes 1544 | tf_op jit(solution)/shard_map/ppermute | solution.py:19
  29.3 58.5 %collective-permute-start.2 = (f32[1,128]{1,0:T(1,128)}, f32[1,128]{1,0:T(1,128)}, u32[]{:S(2)}, u32[]{:S(2)}) collective-permute-start(f32[1,128]{1,0:T(1,128)} %slice.458), channel_id=1, source_target_pairs={{0,1},{1,2},{2,3},{3,4},{4,5},{5,6},{6,7},{7,0},{8,9},{9,10},{10,1... | collective-permute-start | bytes 1544 | tf_op jit(solution)/shard_map/ppermute | solution.py:18
  54.7 7.1 %copy-start.60 = (f32[512]{0:T(512)S(1)}, f32[512]{0:T(512)}, u32[]{:S(2)}) copy-start(f32[512]{0:T(512)} %get-tuple-element.141) | copy-start | bytes 6148
  54.7 7.7 %copy-start.59 = (f32[512]{0:T(512)S(1)}, f32[512]{0:T(512)}, u32[]{:S(2)}) copy-start(f32[512]{0:T(512)} %get-tuple-element.143) | copy-start | bytes 6148
  54.7 7.7 %copy-start.53 = (f32[2,512]{1,0:T(2,128)S(1)}, f32[2,512]{1,0:T(2,128)}, u32[]{:S(2)}) copy-start(f32[2,512]{1,0:T(2,128)} %convolution_bitcast_fusion.6) | copy-start | bytes 12292
  54.7 8.3 %copy-start.56 = (f32[512]{0:T(512)S(1)}, f32[512]{0:T(512)}, u32[]{:S(2)}) copy-start(f32[512]{0:T(512)} %get-tuple-element.142) | copy-start | bytes 6148
  103.1 38.1 %copy-start.61 = (f32[512]{0:T(512)S(1)}, f32[512]{0:T(512)}, u32[]{:S(2)}) copy-start(f32[512]{0:T(512)} %broadcast_multiply_fusion.3) | copy-start | bytes 6148
  103.2 66.2 %copy-start.49 = (f32[3,512]{1,0:T(4,128)S(1)}, f32[3,512]{1,0:T(4,128)}, u32[]{:S(2)}) copy-start(f32[3,512]{1,0:T(4,128)} %scatter-add.15) | copy-start | bytes 18436
  103.2 138.5 %all-reduce.56.cloned.1.call-start = ((), (), s32[]{:S(2)}) async-start(), calls=%async_computation.1 | async-start | bytes 4194304 | tf_op jit(solution)/shard_map/psum | solution.py:218
  141.9 32.4 %copy-start.7 = (f32[1,128,512]{2,1,0:T(8,128)S(1)}, f32[1,128,512]{2,1,0:T(8,128)}, u32[]{:S(2)}) copy-start(f32[1,128,512]{2,1,0:T(8,128)} %copy-done.5) | copy-start | bytes 786436
  141.9 32.4 %copy-start.16 = (f32[1,128,512]{2,1,0:T(8,128)S(1)}, f32[1,128,512]{2,1,0:T(8,128)}, u32[]{:S(2)}) copy-start(f32[1,128,512]{2,1,0:T(8,128)} %copy-done.15) | copy-start | bytes 786436
  169.4 5.9 %copy-start.4 = (f32[1,128,512]{2,1,0:T(8,128)S(1)}, f32[1,128,512]{2,1,0:T(8,128)}, u32[]{:S(2)}) copy-start(f32[1,128,512]{2,1,0:T(8,128)} %copy-done.3) | copy-start | bytes 786436
  169.4 5.9 %copy-start.14 = (f32[1,128,512]{2,1,0:T(8,128)S(1)}, f32[1,128,512]{2,1,0:T(8,128)}, u32[]{:S(2)}) copy-start(f32[1,128,512]{2,1,0:T(8,128)} %copy-done.13) | copy-start | bytes 786436
  169.4 5.9 %copy-start.67 = (f32[2,128,1]{1,0,2:T(2,128)S(1)}, f32[2,128,1]{1,0,2:T(2,128)}, u32[]{:S(2)}) copy-start(f32[2,128,1]{1,0,2:T(2,128)} %reshape.1855) | copy-start | bytes 3076
  169.4 6.3 %copy-start.69 = (f32[1,512]{1,0:T(1,128)S(1)}, f32[1,512]{1,0:T(1,128)}, u32[]{:S(2)}) copy-start(f32[1,512]{1,0:T(1,128)} %get-tuple-element.162) | copy-start | bytes 6148
  169.4 6.3 %copy-start.70 = (f32[1,512]{1,0:T(1,128)S(1)}, f32[1,512]{1,0:T(1,128)}, u32[]{:S(2)}) copy-start(f32[1,512]{1,0:T(1,128)} %get-tuple-element.163) | copy-start | bytes 6148
  169.5 6.8 %copy-start.66 = (f32[1,512,1]{1,0,2:T(1,128)S(1)}, f32[1,512,1]{1,0,2:T(1,128)}, u32[]{:S(2)}) copy-start(f32[1,512,1]{1,0,2:T(1,128)} %fusion.145) | copy-start | bytes 6148
  169.5 7.4 %copy-start.55 = (f32[512]{0:T(512)S(1)}, f32[512]{0:T(512)}, u32[]{:S(2)}) copy-start(f32[512]{0:T(512)} %slice_reduce_fusion) | copy-start | bytes 6148
  169.5 8.0 %copy-start.12 = (bf16[2,128,512]{2,1,0:T(8,128)(2,1)S(1)}, bf16[2,128,512]{2,1,0:T(8,128)(2,1)}, u32[]{:S(2)}) copy-start(bf16[2,128,512]{2,1,0:T(8,128)(2,1)} %copy-done.11) | copy-start | bytes 786436
  169.5 8.0 %copy-start.29 = (bf16[1,128,512]{2,1,0:T(8,128)(2,1)S(1)}, bf16[1,128,512]{2,1,0:T(8,128)(2,1)}, u32[]{:S(2)}) copy-start(bf16[1,128,512]{2,1,0:T(8,128)(2,1)} %copy-done.28) | copy-start | bytes 393220
  (49 other events, 94.3 us)
Sparse Core Ops, SparseCore 0:
  103.3 66.0 all-reduce.53
  172.5 69.1 all-reduce.55
